TPU v7x, 32 devices: a whole 2x2x4 slice. The times are simulated.
32 devices in a mesh: row: 8 (over y, x, core), col: 4 (over z).
Axes of the slice: x: 2, y: 2, z: 4, core: 2. Of those that a mesh axis runs over, the one named last changes fastest.
Arguments:
- relief: float32 [3, 2048, 4096], P(None, 'row', 'col'), may hold values from -8 to 8
Outputs:
- level_one: float32 [3, 1024, 2048], P(None, 'row', 'col')
- level_two: float32 [3, 512, 1024], P(None, 'row', 'col')
- level_three: float32 [3, 256, 512], P(None, 'row', 'col')
- level_four: float32 [3, 128, 256], P(None, 'row', 'col')
All inputs are finite; a program needn't handle non-finite values.
Results may differ from a plain program's by a relative error of at most 0.00002.
Values sent between devices are 32-bit elements; how exact they have to be, the bound alone decides.
No kernel may reach another device: no remote copies, remote signals or barrier semaphores. Data moves between devices by JAX's collectives and lax.ppermute only.
A program may use at most 64 MiB of HBM per device.

v0:
```python
import functools

import jax
import jax.numpy as jnp
from jax import lax
from jax.experimental import pallas as pl
from jax.experimental.pallas import tpu as pltpu
from jax.sharding import PartitionSpec as P


F32 = jnp.float32
BF16 = jnp.bfloat16
FAR = 1 << 20
LEVELS = 4
LIMIT = 24_000_000
VMEM = pl.BlockSpec(memory_space=pltpu.VMEM)
PAD = 8
TAIL = 24


def lanes_of(cols):
    return (cols + 3 + 127) // 128 * 128


def iota(shape, dim):
    return lax.broadcasted_iota(jnp.int32, shape, dim)


def band(source, target):
    far = jnp.abs(source - 2 * target)
    return jnp.where(far == 0, 6 / 256, jnp.where(far == 1, 4 / 256, jnp.where(far == 2, 1 / 256, 0.0))).astype(F32)


def fill_blocks(mats, first, last):
    source, lane = iota((256, 256), 0), iota((256, 256), 1)
    target = jnp.where(lane <= 128, lane, jnp.where(lane == 255, -1, FAR))
    value = band(source, target)
    inside = value.astype(BF16)
    for i in range(4):
        mats[i] = inside
    source, target = iota((16, 128), 0), iota((16, 128), 1)
    mirror = jnp.where(source >= 1, band(-source, target), 0.0)
    start = (value[:16, :128] + first * mirror).astype(BF16)
    source = source + 240
    mirror = jnp.where(source == 254, band(source + 2, target), 0.0)
    end = (value[240:, :128] + last * mirror).astype(BF16)
    for i in (1, 3):
        mats[i, :16, :128] = start
    for i in (2, 3):
        mats[i, 240:, :128] = end


def rim_matrix(first, last):
    source, lane = iota((128, 256), 0), iota((128, 256), 1)
    after = source < 64
    col = jnp.where(after, 512 + source, source - 128)
    own = jnp.where(lane < 2, 256 + lane, jnp.where(lane == 127, -1, FAR))
    other = jnp.where(lane == 128, 0, jnp.where(lane == 255, 255, FAR))
    value = band(col, jnp.where(lane < 128, own, other))
    keep = jnp.where(after, 1.0 - last, 1.0 - first)
    return (value * keep).astype(BF16)


def last_matrix(cols, first, last):
    source, lane = iota((2 * cols, cols), 0), iota((2 * cols, cols), 1)
    half = cols // 2
    col = jnp.where(source < cols + cols // 2, source, source - 2 * cols)
    target = jnp.where(lane < half + 2, lane, jnp.where(lane == cols - 1, -1, FAR))
    value = band(col, target)
    value += first * jnp.where((source >= 1) & (source < cols), band(-source, target), 0.0)
    value += last * jnp.where(source == cols - 2, band(source + 2, target), 0.0)
    keep = jnp.where(col < 0, 1.0 - first, jnp.where(col >= cols, 1.0 - last, 1.0))
    return (value * keep).astype(BF16)


def split_dot(value, matrix):
    high = value.astype(BF16)
    low = (value - high.astype(F32)).astype(BF16)
    size = value.shape[0]
    if size > 80:
        return jnp.dot(
            jnp.concatenate([high, low], 1), jnp.concatenate([matrix, matrix], 0),
            preferred_element_type=F32,
        )
    both = jnp.dot(jnp.concatenate([high, low], 0), matrix, preferred_element_type=F32)
    return both[:size] + both[size:]


def columns(tiles, cols, matrices):
    blocks = cols // 256
    rim = len(tiles) > 2 * blocks
    parts = []
    for t in range(blocks):
        index = (1 if t == 0 else 0) + (2 if t == blocks - 1 else 0)
        value = jnp.concatenate(tiles[2 * t:2 * t + 2], 1)
        parts.append(split_dot(value, matrices[index][...]))
    near = iota((tiles[0].shape[0], 128), 1) < 64
    edges = [p[:, 128:] for p in parts]
    if rim:
        around = split_dot(tiles[-1], matrices[4][...])
        edges.append(around[:, 128:])
    else:
        edges.append(jnp.zeros_like(edges[0]))
    out = [
        parts[t][:, :128] + jnp.where(near, edges[t - 1], edges[t + 1])
        for t in range(blocks)
    ]
    outer = jnp.where(near, edges[blocks - 1], edges[0])
    if rim:
        outer = outer + around[:, :128]
    return out + [outer]


def rows(ref, extent):
    half = extent // 2

    def reduced(start, size):
        e = [ref[pl.ds(start + t, size, stride=2), :] for t in range(5)]
        return (e[0] + e[4]) + 4.0 * (e[1] + e[3]) + 6.0 * e[2]

    main = reduced(PAD - 2, half)
    below = reduced(PAD - 2 + extent, 8)
    above = 4.0 * ref[PAD - 1:PAD, :] + ref[PAD:PAD + 1, :]
    return jnp.concatenate([main, jnp.where(iota(below.shape, 0) == 7, above, below)], 0)


def close(ref, extent, first, last):
    @pl.when(first)
    def _():
        ref[:, PAD - 2:PAD - 1, :] = ref[:, PAD + 2:PAD + 3, :]
        ref[:, PAD - 1:PAD, :] = ref[:, PAD + 1:PAD + 2, :]

    @pl.when(last)
    def _():
        ref[:, PAD + extent:PAD + extent + 1, :] = ref[:, PAD + extent - 2:PAD + extent - 1, :]


def slots(bands, m):
    place, tiles = {}, 0
    for k in range(2, LEVELS + 1):
        for t in range(lanes_of(m >> k) // 128):
            for b in range(bands):
                place[k, t, b] = tiles, 2 * b
            tiles += 1
    free = [(j, r) for j in range(tiles) for r in range(2 * bands, 8)]
    for t in range(lanes_of(m >> 1) // 128):
        for b in range(bands):
            if not free:
                free = [(tiles, r) for r in range(8)]
                tiles += 1
            place[1, t, b] = free.pop(0)
    return place, tiles


HEAD, FOOT = 16, 32


def edge_kernel(
    shape, counts, x_hbm, send_e, send_o, s0, mats, rim_mat, end_mat,
    e1, e2, e3, down, up, sems,
):
    bands, n, m = shape
    row, col = lax.axis_index("row"), lax.axis_index("col")
    top, bottom = row == 0, row == counts[0] - 1

    def load(start, size, t, sem):
        return pltpu.make_async_copy(
            x_hbm.at[:, pl.ds(start, size), pl.ds(128 * t, 128)],
            s0.at[:, t, pl.ds(PAD + start, size), :], sem,
        )

    def wait(size, sem):
        whole = x_hbm.at[:, pl.ds(0, size), :]
        pltpu.make_async_copy(whole, whole, sem).wait()

    for t in range(m // 128):
        load(0, HEAD, t, sems.at[0]).start()
        load(n - FOOT, FOOT, t, sems.at[0]).start()
    for t in range(m // 128):
        load(HEAD, n - HEAD - FOOT, t, sems.at[1]).start()
    left = jnp.where(col == 0, 1.0, 0.0).astype(F32)
    right = jnp.where(col == counts[1] - 1, 1.0, 0.0).astype(F32)
    fill_blocks(mats, left, right)
    rim_mat[...] = rim_matrix(left, right)
    end_mat[...] = last_matrix(end_mat.shape[1], left, right)
    matrices = [mats.at[i] for i in range(4)] + [rim_mat]
    s0[:, :, 0:PAD, :] = jnp.zeros(s0.shape[:2] + (PAD, 128), F32)
    s0[:, :, PAD + n:, :] = jnp.zeros(s0.shape[:2] + (TAIL, 128), F32)
    down[...] = jnp.zeros_like(down)
    up[...] = jnp.zeros_like(up)
    for ref, filled in zip((e1, e2, e3), (24, 16, 16)):
        for b in range(bands):
            ref[:, 40 * b:40 * b + 8, :] = jnp.zeros((ref.shape[0], 8, 128), F32)
            rest = 32 - filled
            ref[:, 40 * (b + 1) - rest:40 * (b + 1), :] = jnp.zeros((ref.shape[0], rest, 128), F32)
    wait(HEAD + FOOT, sems.at[0])
    place, _ = slots(bands, m)
    for k, ref in enumerate((s0, e1, e2, e3)):
        head, foot, size = ((PAD - 4, PAD + n - FOOT, 16), (5, 17, 8), (5, 16, 8), (5, 16, 8))[k]

        def reduced(b, t, start, size):
            lines = [pl.ds(start + i + (40 * b if k else 0), size, stride=2) for i in range(5)]
            e = [ref[t, line, :] if k else ref[b, t, line, :] for line in lines]
            return (e[0] + e[4]) + 4.0 * (e[1] + e[3]) + 6.0 * e[2]

        tiles = [
            jnp.concatenate(
                [
                    part for b in range(bands) for part in (
                        reduced(b, t, head, 8), reduced(b, t, foot, size)
                    )
                ],
                0,
            )
            for t in range(ref.shape[0] if k else m // 128)
        ]
        if k < LEVELS - 1:
            tiles = columns(tiles, m >> k, matrices)
        else:
            tiles = [split_dot(jnp.concatenate(tiles, 1), end_mat[...])]
        held = 8 + size
        first, count = ((23, 1), (14, 2), (10, 2), (8, 2))[k]
        for t, tile in enumerate(tiles):
            for b in range(bands):
                if k < LEVELS - 1:
                    (e1, e2, e3)[k][t, 40 * b + 8:40 * b + 8 + held, :] = tile[held * b:held * b + held]
                spot, line = place[k + 1, t, b]
                wide = pl.ds(128 * spot, 128)
                down[line:line + count, wide] = tile[held * b + first:held * b + first + count]
                up[line:line + 1, wide] = tile[held * b:held * b + 1]
    lower_part = jnp.where(bottom, 0.0, down[...])
    upper_part = jnp.where(top, 0.0, up[...])
    even = (row & 1) == 0
    send_e[...] = jnp.where(even, lower_part, upper_part)
    send_o[...] = jnp.where(even, upper_part, lower_part)
    wait(n - HEAD - FOOT, sems.at[1])
    for b in range(bands):
        close(s0.at[b], n, top, bottom)


def pyramid_kernel(
    shape, counts, s0, mats, rim_mat, end_mat, one, two, three, four, rim_a, rim_b, s1, s2, s3,
):
    bands, n, m = shape
    row = lax.axis_index("row")
    top, bottom = row == 0, row == counts[0] - 1
    matrices = [mats.at[i] for i in range(4)] + [rim_mat]
    fields, outs = [s0, s1, s2, s3], [one, two, three, four]
    sub = iota((8, 128), 0)

    def store(k, b, t, tile):
        half = n >> (k + 1)
        tail, after = tile[half:], fields[k + 1]
        after[b, t, PAD:PAD + half, :] = tile[:half]
        after[b, t, 0:PAD, :] = jnp.where(sub == 7, tail, 0.0)
        after[b, t, PAD + half:PAD + half + 8, :] = jnp.where(sub < 2, tail, 0.0)
        after[b, t, PAD + half + 8:, :] = jnp.zeros((TAIL - 8, 128), F32)
        if 128 * t < outs[k].shape[2]:
            outs[k][b, :, 128 * t:128 * t + 128] = tile[:half]
        elif k == 0:
            rim_a[b] = tile[:half]

    def level_one(b, _):
        tiles = columns([rows(s0.at[b, t], n) for t in range(m // 128)], m, matrices)
        for t, tile in enumerate(tiles):
            store(0, b, t, tile)
        return 0

    lax.fori_loop(0, bands, level_one, 0)
    start = 0
    for k in range(1, LEVELS):
        extent, cols = n >> k, m >> k
        half = extent // 2
        for b in range(bands):
            close(fields[k].at[b], extent, top, bottom)
        tiles = [
            jnp.concatenate([rows(fields[k].at[b, t], extent) for b in range(bands)], 0)
            for t in range(fields[k].shape[1])
        ]
        if k < LEVELS - 1:
            tiles = columns(tiles, cols, matrices)
        else:
            tiles = [split_dot(jnp.concatenate(tiles, 1), end_mat[...])]
        for b in range(bands):
            parts = [tile[(half + 8) * b:(half + 8) * (b + 1)] for tile in tiles]
            body = parts[-1][:half]
            if k < LEVELS - 1:
                for t, tile in enumerate(parts):
                    store(k, b, t, tile)
            else:
                four[b] = body[:, :cols // 2]
                body = jnp.where(iota(body.shape, 1) < 2, pltpu.roll(body, 128 - cols // 2, 1), body)
            rim_b[b, start:start + half, :] = body
        start += half
    rim_b[:, start:, :] = jnp.zeros((bands, 128 - start, 128), F32)


def from_rows(got_e, got_o):
    even = (lax.axis_index("row") & 1) == 0
    e, o = got_e[...], got_o[...]
    return jnp.where(even, o, e), jnp.where(even, e, o)


def row_parts(above, below, place, k, t, b):
    spot, line = place[k, t, b]
    head, foot = (part[:, 128 * spot:128 * spot + 128] for part in (above, below))
    sub = iota(head.shape, 0)
    head = pltpu.roll(head, 8 - line, 0) if line else head
    foot = pltpu.roll(foot, 7 - line, 0) if line < 7 else foot
    return jnp.where(sub < (1 if k == 1 else 2), head, 0.0), jnp.where(sub == 7, foot, 0.0)


def segments(n):
    out, start = [], 0
    for k in range(2, LEVELS + 1):
        out.append((k, start, n >> k))
        start += n >> k
    return out


def rim_kernel(
    shape, counts, rim_a, rim_b, got_e, got_o, send_0, send_1, send_2, tile_a, tile_b
):
    bands, n, m = shape
    above, below = from_rows(got_e, got_o)
    place, _ = slots(bands, m)

    def rim_of(k, b):
        parts = row_parts(above, below, place, k, (m >> k) // 128, b)
        if (m >> k) < 128:
            parts = [jnp.where(iota(p.shape, 1) < 2, pltpu.roll(p, 128 - (m >> k), 1), p) for p in parts]
        return parts

    sub = iota((16, 128), 0)
    to_right, to_left = jnp.zeros((16, 128), F32), jnp.zeros((16, 128), F32)
    for b in range(bands):
        half = n // 2
        tile_a[b] = rim_a[b]
        tile_b[b] = rim_b[b]
        for ref, k, first, size in [(tile_a, 1, 0, half)] + [(tile_b, k, s, z) for k, s, z in segments(n)]:
            head, foot = rim_of(k, b)
            ref[b, first:first + 8, :] += head
            ref[b, first + size - 8:first + size, :] += foot
        a = jnp.transpose(tile_a[b])
        c = jnp.transpose(tile_b[b])
        to_right = jnp.where(sub == 4 * b, a[0:1], to_right)
        to_right = jnp.where(sub == 4 * b + 1, c[0:1], to_right)
        to_right = jnp.where(sub == 4 * b + 2, c[1:2], to_right)
        to_left = jnp.where(sub == 4 * b, a[127:128], to_left)
        to_left = jnp.where(sub == 4 * b + 1, c[127:128], to_left)
    col = lax.axis_index("col")
    to_right = jnp.where(col == counts[1] - 1, 0.0, to_right)
    to_left = jnp.where(col == 0, 0.0, to_left)
    for k, send in enumerate((send_0, send_1, send_2)):
        left = jnp.where((col + 2) % 3 == k, to_left, 0.0)
        send[...] = jnp.where(col % 3 == k, to_right, left)


def settle_kernel(
    shape, one, two, three, four, row_e, row_o, out, done_one, done_two, done_three, done_four, inner, sems
):
    bands, n, m = shape
    above, below = from_rows(row_e, row_o)
    place, _ = slots(bands, m)
    tiles = (m >> 1) // 128
    copies = []
    for b in range(bands):
        for k, (field, done) in enumerate(zip((one, two, three, four), (done_one, done_two, done_three, done_four)), 1):
            cols, size = m >> k, n >> k
            wide = min(cols, 128)
            for t in range(cols // wide):
                at, to, ref = pl.ds(wide * t, wide), pl.ds(wide * t, wide), done
                if k == 1:
                    if 0 < t < tiles - 1:
                        ref, to = inner, pl.ds(128 * (t - 1), 128)
                    else:
                        to = pl.ds(128 * min(t, 1), 128)
                head, foot = row_parts(above, below, place, k, t, b)
                ref[b, 0:8, to] = field[b, 0:8, at] + head[:, :wide]
                if size > 16:
                    ref[b, 8:size - 8, to] = field[b, 8:size - 8, at]
                ref[b, size - 8:size, to] = field[b, size - 8:size, at] + foot[:, :wide]
            if k == 1:
                copy = pltpu.make_async_copy(
                    inner.at[b], out.at[b, :, pl.ds(128, 128 * (tiles - 2))], sems.at[b]
                )
                copy.start()
                copies.append(copy)
    for copy in copies:
        copy.wait()


def finish_kernel(
    shape, _, one, two, three, four, col_0, col_1, col_2,
    out_one, out_two, out_three, out_four, tile_a, tile_b, new_one, new_two, new_three, new_four, sems,
):
    bands, n, m = shape
    turn = lax.axis_index("col") % 3
    got = [col_0[...], col_1[...], col_2[...]]
    after = jnp.where(turn == 0, got[0], jnp.where(turn == 1, got[1], got[2]))
    before = jnp.where(turn == 0, got[2], jnp.where(turn == 1, got[0], got[1]))
    fields, news = [one, two, three, four], [new_one, new_two, new_three, new_four]
    outs = [out_one, out_two, out_three, out_four]
    tile_a[...] = jnp.zeros_like(tile_a)
    tile_b[...] = jnp.zeros_like(tile_b)
    lane = iota((128, 128), 1)
    copies = []

    def send(source, target):
        copy = pltpu.make_async_copy(source, target, sems.at[len(copies)])
        copy.start()
        copies.append(copy)

    def add(k, b, part):
        cols, size = m >> k, part.shape[0]
        wide = min(cols, 128)
        spot = lane[:size, :wide]
        part = part[:, :wide]
        low, high = jnp.where(spot < 2, part, 0.0), jnp.where(spot == wide - 1, part, 0.0)
        count = min(cols // wide, 2)
        for t in range(count):
            at = pl.ds(wide * t, wide)
            value = fields[k - 1][b, :, at]
            if t == 0:
                value = value + low
            if t == count - 1:
                value = value + high
            news[k - 1][b, :, at] = value

    for b in range(bands):
        tile_a[b, 0:1, :] = before[4 * b:4 * b + 1]
        tile_a[b, 127:128, :] = after[4 * b:4 * b + 1]
        tile_b[b, 0:2, :] = before[4 * b + 1:4 * b + 3]
        tile_b[b, 127:128, :] = after[4 * b + 1:4 * b + 2]
        tile_b[b, 63:64, :] = after[4 * b + 1:4 * b + 2]
    for b in range(bands):
        add(1, b, jnp.transpose(tile_a[b]))
        for t, at in enumerate((0, (m >> 1) - 128)):
            send(new_one.at[b, :, pl.ds(128 * t, 128)], out_one.at[b, :, pl.ds(at, 128)])
    for b in range(bands):
        c = jnp.transpose(tile_b[b])
        for k, first, size in segments(n):
            add(k, b, c[first:first + size])
    for new, out in zip(news[1:], outs[1:]):
        send(new, out)
    for copy in copies:
        copy.wait()


def swap(values, axis, counts):
    sizes = [counts[name] for name in ("row", "col")]
    along = ("row", "col").index(axis)
    out = []
    for k, value in enumerate(values):
        moves = []
        for i in range(sizes[0] * sizes[1]):
            place = list(divmod(i, sizes[1]))
            target = list(place)
            here = place[along]
            if here % len(values) == k and here + 1 < sizes[along]:
                target[along] += 1
            elif (here - 1) % len(values) == k and here > 0:
                target[along] -= 1
            elif (place[1 - along] ^ 1) < sizes[1 - along]:
                target[1 - along] ^= 1
            else:
                continue
            moves.append((i, target[0] * sizes[1] + target[1]))
        out.append(lax.ppermute(value, ("row", "col"), moves))
    return out


def solution(mesh):
    counts = (mesh.shape["row"], mesh.shape["col"])

    def local(relief):
        shape = bands, n, m = relief.shape
        levels = [jax.ShapeDtypeStruct((bands, n >> k, m >> k), F32) for k in range(1, LEVELS + 1)]
        width = 128 * slots(bands, m)[1]
        row_part = jax.ShapeDtypeStruct((8, width), F32)
        col_part = jax.ShapeDtypeStruct((16, 128), F32)
        rim = jax.ShapeDtypeStruct((bands, 128, 128), F32)
        tall = [
            jax.ShapeDtypeStruct((bands, (lanes_of(m >> k) if k else m) // 128, PAD + (n >> k) + TAIL, 128), F32)
            for k in range(LEVELS)
        ]
        send_e, send_o, field, *mats = pl.pallas_call(
            functools.partial(edge_kernel, shape, counts),
            out_shape=[
                row_part, row_part, tall[0],
                jax.ShapeDtypeStruct((4, 256, 256), BF16),
                jax.ShapeDtypeStruct((128, 256), BF16),
                jax.ShapeDtypeStruct((m >> 2, m >> 3), BF16),
            ],
            in_specs=[pl.BlockSpec(memory_space=pltpu.HBM)],
            out_specs=[VMEM] * 6,
            scratch_shapes=[
                pltpu.VMEM((lanes_of(m >> k) // 128, bands * 40, 128), F32) for k in range(1, LEVELS)
            ] + [
                pltpu.VMEM((8, width), F32),
                pltpu.VMEM((8, width), F32),
                pltpu.SemaphoreType.DMA((2,)),
            ],
            compiler_params=pltpu.CompilerParams(vmem_limit_bytes=LIMIT),
            name="edge",
        )(pltpu.with_memory_space_constraint(relief, pltpu.HBM))
        *own, rim_a, rim_b = pl.pallas_call(
            functools.partial(pyramid_kernel, shape, counts),
            out_shape=levels + [rim, rim],
            in_specs=[VMEM] * 4,
            out_specs=[VMEM] * 6,
            scratch_shapes=[pltpu.VMEM(t.shape, F32) for t in tall[1:]],
            compiler_params=pltpu.CompilerParams(vmem_limit_bytes=LIMIT),
            cost_estimate=pl.CostEstimate(flops=8_000_000_000, bytes_accessed=0, transcendentals=0),
            name="pyramid",
        )(field, *mats)
        row_e, row_o = swap((send_e, send_o), "row", mesh.shape)
        sends = pl.pallas_call(
            functools.partial(rim_kernel, shape, counts),
            out_shape=[col_part] * 3,
            in_specs=[VMEM] * 4,
            out_specs=[VMEM] * 3,
            scratch_shapes=[pltpu.VMEM((bands, 128, 128), F32)] * 2,
            compiler_params=pltpu.CompilerParams(vmem_limit_bytes=4 << 20),
            name="rim",
        )(rim_a, rim_b, row_e, row_o)
        cols = swap(sends, "col", mesh.shape)
        ends = jax.ShapeDtypeStruct((bands, n >> 1, 256), F32)
        hbm = pl.BlockSpec(memory_space=pltpu.HBM)
        out, *done = pl.pallas_call(
            functools.partial(settle_kernel, shape),
            out_shape=[levels[0], ends] + levels[1:],
            in_specs=[VMEM] * 6,
            out_specs=[hbm] + [VMEM] * 4,
            scratch_shapes=[
                pltpu.VMEM((bands, n >> 1, (m >> 1) - 256), F32), pltpu.SemaphoreType.DMA((bands,)),
            ],
            compiler_params=pltpu.CompilerParams(vmem_limit_bytes=8 << 20),
            cost_estimate=pl.CostEstimate(flops=2_000_000_000, bytes_accessed=0, transcendentals=0),
            name="settle",
        )(*own, row_e, row_o)
        return tuple(pl.pallas_call(
            functools.partial(finish_kernel, shape),
            out_shape=levels,
            in_specs=[hbm] + [VMEM] * 7,
            out_specs=[hbm] * 4,
            scratch_shapes=[pltpu.VMEM((bands, 128, 128), F32)] * 2 + [
                pltpu.VMEM(level.shape, F32) for level in [ends] + levels[1:]
            ] + [pltpu.SemaphoreType.DMA((2 * bands + LEVELS - 1,))],
            input_output_aliases={0: 0},
            compiler_params=pltpu.CompilerParams(vmem_limit_bytes=8 << 20),
            name="finish",
        )(out, *done, *cols))

    placed = P(None, "row", "col")
    return jax.shard_map(
        local, mesh=mesh, in_specs=(placed,), out_specs=(placed,) * LEVELS, check_vma=False
    )
```

profile of v0, /device:TPU:0, one launch (start us, length us, event | category | flops | bytes accessed | tf_op | source)
XLA Modules:
  0.0 13.0 jit_solution(6550072051392183157)
XLA Ops:
  0.6 2.1 %edge.1 = (f32[8,896]{1,0:T(8,128)S(1)}, f32[8,896]{1,0:T(8,128)S(1)}, f32[3,8,288,128]{3,2,1,0:T(8,128)S(1)}, bf16[4,256,256]{2,1,0:T(8,128)(2,1)S(1)}, bf16[12...) custom-call(f32[3,256,1024]{2,1,0:T(8,128)} %x_hbm.1), custom_call_target="tpu_custom_call" | custom-call | tf_op jit(solution)/shard_map/edge/pallas_call | solution.py:487
  2.7 0.5 %collective-permute-start = (f32[8,896]{1,0:T(8,128)S(1)}, f32[8,896]{1,0:T(8,128)S(1)}, u32[]{:S(2)}, u32[]{:S(2)}) collective-permute-start(f32[8,896]{1,0:T(8,128)S(1)} %get-tuple-element.32), channel_id=1, source_target_pairs={{0,4},{1,5},{2,6},{3,7},{4,0},{5,1},{6,2},{7,3},{8,12},{9,13},{10,... | collective-permute-start | bytes 86024 | tf_op jit(solution)/shard_map/ppermute | solution.py:469
  3.2 2.7 %collective-permute-start.1 = (f32[8,896]{1,0:T(8,128)S(1)}, f32[8,896]{1,0:T(8,128)S(1)}, u32[]{:S(2)}, u32[]{:S(2)}) collective-permute-start(f32[8,896]{1,0:T(8,128)S(1)} %get-tuple-element.33), channel_id=1, source_target_pairs={{0,1},{1,0},{2,3},{3,2},{4,8},{5,9},{6,10},{7,11},{8,4},{9,5},{10,... | collective-permute-start | bytes 86024 | tf_op jit(solution)/shard_map/ppermute | solution.py:469
  5.9 2.2 %pyramid.1 = (f32[3,128,512]{2,1,0:T(8,128)S(1)}, f32[3,64,256]{2,1,0:T(8,128)S(1)}, f32[3,32,128]{2,1,0:T(8,128)S(1)}, f32[3,16,64]{2,1,0:T(8,128)S(1)}, f32[3,...) custom-call(f32[3,8,288,128]{3,2,1,0:T(8,128)S(1)} %get-tuple-element.24.s0, ...), custom_call_target="tpu_custom_call" | custom-call | flops 8000000000 | tf_op jit(solution)/shard_map/pyramid/pallas_call | solution.py:507
  8.1 0.0 collective-permute-done.row_e.got_e
  8.1 0.0 collective-permute-done.1.row_o.got_o
  8.1 0.2 %rim.1 = (f32[16,128]{1,0:T(8,128)S(1)}, f32[16,128]{1,0:T(8,128)S(1)}, f32[16,128]{1,0:T(8,128)S(1)}) custom-call(f32[3,128,128]{2,1,0:T(8,128)S(1)} %get-tuple-element.39.rim_a, f32[3,128,128]{2,1,0:T(8,128)S(1)} %get-tuple-element.40.rim_b, f32[8,896]{1,0:T(8,128)S(1)} %collective-permute-done.row_e.got_e, f32[8,896]{1,0:T(8,128)S(1)} %collective-permute-done.1.row_o.got_o), custom_call_target="tpu_custom_call" | custom-call | tf_op jit(solution)/shard_map/rim/pallas_call | solution.py:518
  8.3 1.7 %collective-permute-start.2 = (f32[16,128]{1,0:T(8,128)S(1)}, f32[16,128]{1,0:T(8,128)S(1)}, u32[]{:S(2)}, u32[]{:S(2)}) collective-permute-start(f32[16,128]{1,0:T(8,128)S(1)} %get-tuple-element.41), channel_id=1, source_target_pairs={{0,1},{1,0},{2,6},{3,7},{4,5},{5,4},{6,2},{7,3},{8,9},{9,8},{10,14... | collective-permute-start | bytes 24584 | tf_op jit(solution)/shard_map/ppermute | solution.py:469
  10.0 0.0 collective-permute-start.3
  10.0 0.5 %collective-permute-start.4 = (f32[16,128]{1,0:T(8,128)S(1)}, f32[16,128]{1,0:T(8,128)S(1)}, u32[]{:S(2)}, u32[]{:S(2)}) collective-permute-start(f32[16,128]{1,0:T(8,128)S(1)} %get-tuple-element.43), channel_id=1, source_target_pairs={{0,4},{1,5},{2,3},{3,2},{4,0},{5,1},{6,7},{7,6},{8,12},{9,13},{10,... | collective-permute-start | bytes 24584 | tf_op jit(solution)/shard_map/ppermute | solution.py:469
  10.6 0.8 %settle.1 = (f32[3,128,512]{2,1,0:T(8,128)}, f32[3,128,256]{2,1,0:T(8,128)S(1)}, f32[3,64,256]{2,1,0:T(8,128)S(1)}, f32[3,32,128]{2,1,0:T(8,128)S(1)}, f32[3,16,64]{2,1,0:T(8,128)S(1)}) custom-call(f32[3,128,512]{2,1,0:T(8,128)S(1)} %get-tuple-element.28.one, f32[3,64,256]{2,1,0:T(8,128)S(1)} %get-tuple-element.29.two, ...), custom_call_target="tpu_custom_call" | custom-call | flops 2000000000 | tf_op jit(solution)/shard_map/settle/pallas_call | solution.py:530
  11.3 0.7 %collective-permute-done.2.col_0 = f32[16,128]{1,0:T(8,128)S(1)} collective-permute-done((f32[16,128]{1,0:T(8,128)S(1)}, f32[16,128]{1,0:T(8,128)S(1)}, u32[]{:S(2)}, u32[]{:S(2)}) %collective-permute-start.2) | collective-permute-done | bytes 8224 | tf_op jit(solution)/shard_map/ppermute | solution.py:469
  12.0 0.0 collective-permute-done.3.col_1
  12.0 0.0 collective-permute-done.4.col_2
  12.0 1.0 %finish.1 = (f32[3,128,512]{2,1,0:T(8,128)}, f32[3,64,256]{2,1,0:T(8,128)}, f32[3,32,128]{2,1,0:T(8,128)}, f32[3,16,64]{2,1,0:T(8,128)}) custom-call(f32[3,128,512]{2,1,0:T(8,128)} %get-tuple-element.34._, f32[3,128,256]{2,1,0:T(8,128)S(1)} %get-tuple-element.35.one, f32[3,64,256]{2,1,0:T(8,128)S(1)} %get-tuple-element.36.two, ...), custom_call_target="tpu_custom_call", output_to_operand_aliasing={{0}: (0, {})} | custom-call | tf_op jit(solution)/shard_map/finish/pallas_call | solution.py:542
Async XLA Ops:
  2.7 5.4 %collective-permute-start = (f32[8,896]{1,0:T(8,128)S(1)}, f32[8,896]{1,0:T(8,128)S(1)}, u32[]{:S(2)}, u32[]{:S(2)}) collective-permute-start(f32[8,896]{1,0:T(8,128)S(1)} %get-tuple-element.32), channel_id=1, source_target_pairs={{0,4},{1,5},{2,6},{3,7},{4,0},{5,1},{6,2},{7,3},{8,12},{9,13},{10,... | collective-permute-start | bytes 86024 | tf_op jit(solution)/shard_map/ppermute | solution.py:469
  3.2 4.8 %collective-permute-start.1 = (f32[8,896]{1,0:T(8,128)S(1)}, f32[8,896]{1,0:T(8,128)S(1)}, u32[]{:S(2)}, u32[]{:S(2)}) collective-permute-start(f32[8,896]{1,0:T(8,128)S(1)} %get-tuple-element.33), channel_id=1, source_target_pairs={{0,1},{1,0},{2,3},{3,2},{4,8},{5,9},{6,10},{7,11},{8,4},{9,5},{10,... | collective-permute-start | bytes 86024 | tf_op jit(solution)/shard_map/ppermute | solution.py:469
  8.3 3.7 %collective-permute-start.2 = (f32[16,128]{1,0:T(8,128)S(1)}, f32[16,128]{1,0:T(8,128)S(1)}, u32[]{:S(2)}, u32[]{:S(2)}) collective-permute-start(f32[16,128]{1,0:T(8,128)S(1)} %get-tuple-element.41), channel_id=1, source_target_pairs={{0,1},{1,0},{2,6},{3,7},{4,5},{5,4},{6,2},{7,3},{8,9},{9,8},{10,14... | collective-permute-start | bytes 24584 | tf_op jit(solution)/shard_map/ppermute | solution.py:469
  10.0 2.0 %collective-permute-start.3 = (f32[16,128]{1,0:T(8,128)S(1)}, f32[16,128]{1,0:T(8,128)S(1)}, u32[]{:S(2)}, u32[]{:S(2)}) collective-permute-start(f32[16,128]{1,0:T(8,128)S(1)} %get-tuple-element.42), channel_id=1, source_target_pairs={{0,4},{1,2},{2,1},{3,7},{4,0},{5,6},{6,5},{7,3},{8,12},{9,10},{10,... | collective-permute-start | bytes 24584 | tf_op jit(solution)/shard_map/ppermute | solution.py:469
  10.0 2.0 %collective-permute-start.4 = (f32[16,128]{1,0:T(8,128)S(1)}, f32[16,128]{1,0:T(8,128)S(1)}, u32[]{:S(2)}, u32[]{:S(2)}) collective-permute-start(f32[16,128]{1,0:T(8,128)S(1)} %get-tuple-element.43), channel_id=1, source_target_pairs={{0,4},{1,5},{2,3},{3,2},{4,0},{5,1},{6,7},{7,6},{8,12},{9,13},{10,... | collective-permute-start | bytes 24584 | tf_op jit(solution)/shard_map/ppermute | solution.py:469
where the time goes:
time: 13.2 us; the launch traced here: 13 us
  Pallas kernels  6.24 us (47%)
  starting transfers between devices  5.45 us (41%)
  waiting for transfers between devices  0.68 us (5%)
  between operations  0.67 us (5%)
    ppermute x5, starting transfers between devices, swap(): out.append(lax.ppermute(value, ('row', 'col'), moves))  5.45 us
    pallas_call x1, Pallas kernels, local(): pl.pallas_call(functools.partial(pyramid_kernel, shape, counts), out_shap...  2.17 us
    pallas_call x1, Pallas kernels, local(): pl.pallas_call(functools.partial(edge_kernel, shape, counts), out_shape=[...  2.07 us
    pallas_call x1, Pallas kernels, local(): pl.pallas_call(functools.partial(finish_kernel, shape), out_shape=levels,...  1.02 us
    pallas_call x1, Pallas kernels, local(): pl.pallas_call(functools.partial(settle_kernel, shape), out_shape=[levels...  0.79 us
    ppermute x5, waiting for transfers between devices, swap(): out.append(lax.ppermute(value, ('row', 'col'), moves))  0.68 us
  transfers between devices with their start and end apart: 5, of which 1 were waited for; matrix products, arithmetic and copies ran while one was open for 0% of the time, Pallas kernels for 23%

commit v1 on v0

--- a/solution.py
+++ b/solution.py
@@ -176,8 +176,10 @@
     for t in range(m // 128):
         load(0, HEAD, t, sems.at[0]).start()
         load(n - FOOT, FOOT, t, sems.at[0]).start()
-    for t in range(m // 128):
-        load(HEAD, n - HEAD - FOOT, t, sems.at[1]).start()
+    part = (n - HEAD - FOOT) // 2
+    for i in range(2):
+        for t in range(m // 128):
+            load(HEAD + part * i, part, t, sems.at[1]).start()
     left = jnp.where(col == 0, 1.0, 0.0).astype(F32)
     right = jnp.where(col == counts[1] - 1, 1.0, 0.0).astype(F32)
     fill_blocks(mats, left, right)
@@ -239,13 +241,13 @@
 
 
 def pyramid_kernel(
-    shape, counts, s0, mats, rim_mat, end_mat, one, two, three, four, rim_a, rim_b, s1, s2, s3,
+    shape, counts, s0, mats, rim_mat, end_mat, s1, s2, s3, four, rim_a, rim_b,
 ):
     bands, n, m = shape
     row = lax.axis_index("row")
     top, bottom = row == 0, row == counts[0] - 1
     matrices = [mats.at[i] for i in range(4)] + [rim_mat]
-    fields, outs = [s0, s1, s2, s3], [one, two, three, four]
+    fields = [s0, s1, s2, s3]
     sub = iota((8, 128), 0)
 
     def store(k, b, t, tile):
@@ -255,9 +257,7 @@
         after[b, t, 0:PAD, :] = jnp.where(sub == 7, tail, 0.0)
         after[b, t, PAD + half:PAD + half + 8, :] = jnp.where(sub < 2, tail, 0.0)
         after[b, t, PAD + half + 8:, :] = jnp.zeros((TAIL - 8, 128), F32)
-        if 128 * t < outs[k].shape[2]:
-            outs[k][b, :, 128 * t:128 * t + 128] = tile[:half]
-        elif k == 0:
+        if k == 0 and t == after.shape[1] - 1:
             rim_a[b] = tile[:half]
 
     def level_one(b, _):
@@ -369,17 +369,18 @@
             cols, size = m >> k, n >> k
             wide = min(cols, 128)
             for t in range(cols // wide):
-                at, to, ref = pl.ds(wide * t, wide), pl.ds(wide * t, wide), done
+                to, ref = pl.ds(wide * t, wide), done
                 if k == 1:
                     if 0 < t < tiles - 1:
                         ref, to = inner, pl.ds(128 * (t - 1), 128)
                     else:
                         to = pl.ds(128 * min(t, 1), 128)
                 head, foot = row_parts(above, below, place, k, t, b)
-                ref[b, 0:8, to] = field[b, 0:8, at] + head[:, :wide]
+                own = field.at[b] if k == LEVELS else field.at[b, t, pl.ds(PAD, size), :]
+                ref[b, 0:8, to] = own[0:8, :] + head[:, :wide]
                 if size > 16:
-                    ref[b, 8:size - 8, to] = field[b, 8:size - 8, at]
-                ref[b, size - 8:size, to] = field[b, size - 8:size, at] + foot[:, :wide]
+                    ref[b, 8:size - 8, to] = own[8:size - 8, :]
+                ref[b, size - 8:size, to] = own[size - 8:size, :] + foot[:, :wide]
             if k == 1:
                 copy = pltpu.make_async_copy(
                     inner.at[b], out.at[b, :, pl.ds(128, 128 * (tiles - 2))], sems.at[b]
@@ -506,10 +507,9 @@
         )(pltpu.with_memory_space_constraint(relief, pltpu.HBM))
         *own, rim_a, rim_b = pl.pallas_call(
             functools.partial(pyramid_kernel, shape, counts),
-            out_shape=levels + [rim, rim],
+            out_shape=tall[1:] + [levels[-1], rim, rim],
             in_specs=[VMEM] * 4,
             out_specs=[VMEM] * 6,
-            scratch_shapes=[pltpu.VMEM(t.shape, F32) for t in tall[1:]],
             compiler_params=pltpu.CompilerParams(vmem_limit_bytes=LIMIT),
             cost_estimate=pl.CostEstimate(flops=8_000_000_000, bytes_accessed=0, transcendentals=0),
             name="pyramid",

time: 13.2 us -> 13.2 us (level)
  no operation moved by 1% of the time
where the time goes in v1:
time: 13.2 us; the launch traced here: 13.1 us
  Pallas kernels  6.25 us (47%)
  starting transfers between devices  5.43 us (41%)
  waiting for transfers between devices  0.7 us (5%)
  between operations  0.67 us (5%)
    ppermute x5, starting transfers between devices, swap(): out.append(lax.ppermute(value, ('row', 'col'), moves))  5.43 us
    pallas_call x1, Pallas kernels, local(): pl.pallas_call(functools.partial(pyramid_kernel, shape, counts), out_shap...  2.19 us
    pallas_call x1, Pallas kernels, local(): pl.pallas_call(functools.partial(edge_kernel, shape, counts), out_shape=[...  2.06 us
    pallas_call x1, Pallas kernels, local(): pl.pallas_call(functools.partial(finish_kernel, shape), out_shape=levels,...  1.02 us
    pallas_call x1, Pallas kernels, local(): pl.pallas_call(functools.partial(settle_kernel, shape), out_shape=[levels...  0.78 us
    ppermute x5, waiting for transfers between devices, swap(): out.append(lax.ppermute(value, ('row', 'col'), moves))  0.7 us
  transfers between devices with their start and end apart: 5, of which 1 were waited for; matrix products, arithmetic and copies ran while one was open for 0% of the time, Pallas kernels for 23%

profile of v1, /device:TPU:0, one launch (start us, length us, event | category | flops | bytes accessed | tf_op | source)
XLA Modules:
  0.0 13.1 jit_solution(18116234389651670757)
XLA Ops:
  0.6 2.1 %edge.1 = (f32[8,896]{1,0:T(8,128)S(1)}, f32[8,896]{1,0:T(8,128)S(1)}, f32[3,8,288,128]{3,2,1,0:T(8,128)S(1)}, bf16[4,256,256]{2,1,0:T(8,128)(2,1)S(1)}, bf16[12...) custom-call(f32[3,256,1024]{2,1,0:T(8,128)} %x_hbm.1), custom_call_target="tpu_custom_call" | custom-call | tf_op jit(solution)/shard_map/edge/pallas_call | solution.py:488
  2.7 0.5 %collective-permute-start = (f32[8,896]{1,0:T(8,128)S(1)}, f32[8,896]{1,0:T(8,128)S(1)}, u32[]{:S(2)}, u32[]{:S(2)}) collective-permute-start(f32[8,896]{1,0:T(8,128)S(1)} %get-tuple-element.32), channel_id=1, source_target_pairs={{0,4},{1,5},{2,6},{3,7},{4,0},{5,1},{6,2},{7,3},{8,12},{9,13},{10,... | collective-permute-start | bytes 86024 | tf_op jit(solution)/shard_map/ppermute | solution.py:470
  3.2 2.7 %collective-permute-start.1 = (f32[8,896]{1,0:T(8,128)S(1)}, f32[8,896]{1,0:T(8,128)S(1)}, u32[]{:S(2)}, u32[]{:S(2)}) collective-permute-start(f32[8,896]{1,0:T(8,128)S(1)} %get-tuple-element.33), channel_id=1, source_target_pairs={{0,1},{1,0},{2,3},{3,2},{4,8},{5,9},{6,10},{7,11},{8,4},{9,5},{10,... | collective-permute-start | bytes 86024 | tf_op jit(solution)/shard_map/ppermute | solution.py:470
  5.9 2.2 %pyramid.1 = (f32[3,5,160,128]{3,2,1,0:T(8,128)S(1)}, f32[3,3,96,128]{3,2,1,0:T(8,128)S(1)}, f32[3,2,64,128]{3,2,1,0:T(8,128)S(1)}, f32[3,16,64]{2,1,0:T(8,128)S...) custom-call(f32[3,8,288,128]{3,2,1,0:T(8,128)S(1)} %get-tuple-element.24.s0, ...), custom_call_target="tpu_custom_call" | custom-call | flops 8000000000 | tf_op jit(solution)/shard_map/pyramid/pallas_call | solution.py:508
  8.1 0.0 collective-permute-done.row_e.got_e
  8.1 0.0 collective-permute-done.1.row_o.got_o
  8.1 0.2 %rim.1 = (f32[16,128]{1,0:T(8,128)S(1)}, f32[16,128]{1,0:T(8,128)S(1)}, f32[16,128]{1,0:T(8,128)S(1)}) custom-call(f32[3,128,128]{2,1,0:T(8,128)S(1)} %get-tuple-element.39.rim_a, f32[3,128,128]{2,1,0:T(8,128)S(1)} %get-tuple-element.40.rim_b, f32[8,896]{1,0:T(8,128)S(1)} %collective-permute-done.row_e.got_e, f32[8,896]{1,0:T(8,128)S(1)} %collective-permute-done.1.row_o.got_o), custom_call_target="tpu_custom_call" | custom-call | tf_op jit(solution)/shard_map/rim/pallas_call | solution.py:518
  8.3 1.7 %collective-permute-start.2 = (f32[16,128]{1,0:T(8,128)S(1)}, f32[16,128]{1,0:T(8,128)S(1)}, u32[]{:S(2)}, u32[]{:S(2)}) collective-permute-start(f32[16,128]{1,0:T(8,128)S(1)} %get-tuple-element.41), channel_id=1, source_target_pairs={{0,1},{1,0},{2,6},{3,7},{4,5},{5,4},{6,2},{7,3},{8,9},{9,8},{10,14... | collective-permute-start | bytes 24584 | tf_op jit(solution)/shard_map/ppermute | solution.py:470
  10.0 0.0 collective-permute-start.3
  10.0 0.5 %collective-permute-start.4 = (f32[16,128]{1,0:T(8,128)S(1)}, f32[16,128]{1,0:T(8,128)S(1)}, u32[]{:S(2)}, u32[]{:S(2)}) collective-permute-start(f32[16,128]{1,0:T(8,128)S(1)} %get-tuple-element.43), channel_id=1, source_target_pairs={{0,4},{1,5},{2,3},{3,2},{4,0},{5,1},{6,7},{7,6},{8,12},{9,13},{10,... | collective-permute-start | bytes 24584 | tf_op jit(solution)/shard_map/ppermute | solution.py:470
  10.5 0.8 %settle.1 = (f32[3,128,512]{2,1,0:T(8,128)}, f32[3,128,256]{2,1,0:T(8,128)S(1)}, f32[3,64,256]{2,1,0:T(8,128)S(1)}, f32[3,32,128]{2,1,0:T(8,128)S(1)}, f32[3,16,64]{2,1,0:T(8,128)S(1)}) custom-call(f32[3,5,160,128]{3,2,1,0:T(8,128)S(1)} %get-tuple-element.28.one, f32[3,3,96,128]{3,2,1,0:T(8,128)S(1)} %get-tuple-element.29.two, ...), custom_call_target="tpu_custom_call" | custom-call | flops 2000000000 | tf_op jit(solution)/shard_map/settle/pallas_call | solution.py:530
  11.3 0.7 %collective-permute-done.2.col_0 = f32[16,128]{1,0:T(8,128)S(1)} collective-permute-done((f32[16,128]{1,0:T(8,128)S(1)}, f32[16,128]{1,0:T(8,128)S(1)}, u32[]{:S(2)}, u32[]{:S(2)}) %collective-permute-start.2) | collective-permute-done | bytes 8224 | tf_op jit(solution)/shard_map/ppermute | solution.py:470
  12.0 0.0 collective-permute-done.3.col_1
  12.0 0.0 collective-permute-done.4.col_2
  12.0 1.0 %finish.1 = (f32[3,128,512]{2,1,0:T(8,128)}, f32[3,64,256]{2,1,0:T(8,128)}, f32[3,32,128]{2,1,0:T(8,128)}, f32[3,16,64]{2,1,0:T(8,128)}) custom-call(f32[3,128,512]{2,1,0:T(8,128)} %get-tuple-element.34._, f32[3,128,256]{2,1,0:T(8,128)S(1)} %get-tuple-element.35.one, f32[3,64,256]{2,1,0:T(8,128)S(1)} %get-tuple-element.36.two, ...), custom_call_target="tpu_custom_call", output_to_operand_aliasing={{0}: (0, {})} | custom-call | tf_op jit(solution)/shard_map/finish/pallas_call | solution.py:542
Async XLA Ops:
  2.7 5.4 %collective-permute-start = (f32[8,896]{1,0:T(8,128)S(1)}, f32[8,896]{1,0:T(8,128)S(1)}, u32[]{:S(2)}, u32[]{:S(2)}) collective-permute-start(f32[8,896]{1,0:T(8,128)S(1)} %get-tuple-element.32), channel_id=1, source_target_pairs={{0,4},{1,5},{2,6},{3,7},{4,0},{5,1},{6,2},{7,3},{8,12},{9,13},{10,... | collective-permute-start | bytes 86024 | tf_op jit(solution)/shard_map/ppermute | solution.py:470
  3.2 4.9 %collective-permute-start.1 = (f32[8,896]{1,0:T(8,128)S(1)}, f32[8,896]{1,0:T(8,128)S(1)}, u32[]{:S(2)}, u32[]{:S(2)}) collective-permute-start(f32[8,896]{1,0:T(8,128)S(1)} %get-tuple-element.33), channel_id=1, source_target_pairs={{0,1},{1,0},{2,3},{3,2},{4,8},{5,9},{6,10},{7,11},{8,4},{9,5},{10,... | collective-permute-start | bytes 86024 | tf_op jit(solution)/shard_map/ppermute | solution.py:470
  8.3 3.7 %collective-permute-start.2 = (f32[16,128]{1,0:T(8,128)S(1)}, f32[16,128]{1,0:T(8,128)S(1)}, u32[]{:S(2)}, u32[]{:S(2)}) collective-permute-start(f32[16,128]{1,0:T(8,128)S(1)} %get-tuple-element.41), channel_id=1, source_target_pairs={{0,1},{1,0},{2,6},{3,7},{4,5},{5,4},{6,2},{7,3},{8,9},{9,8},{10,14... | collective-permute-start | bytes 24584 | tf_op jit(solution)/shard_map/ppermute | solution.py:470
  10.0 2.0 %collective-permute-start.3 = (f32[16,128]{1,0:T(8,128)S(1)}, f32[16,128]{1,0:T(8,128)S(1)}, u32[]{:S(2)}, u32[]{:S(2)}) collective-permute-start(f32[16,128]{1,0:T(8,128)S(1)} %get-tuple-element.42), channel_id=1, source_target_pairs={{0,4},{1,2},{2,1},{3,7},{4,0},{5,6},{6,5},{7,3},{8,12},{9,10},{10,... | collective-permute-start | bytes 24584 | tf_op jit(solution)/shard_map/ppermute | solution.py:470
  10.0 2.0 %collective-permute-start.4 = (f32[16,128]{1,0:T(8,128)S(1)}, f32[16,128]{1,0:T(8,128)S(1)}, u32[]{:S(2)}, u32[]{:S(2)}) collective-permute-start(f32[16,128]{1,0:T(8,128)S(1)} %get-tuple-element.43), channel_id=1, source_target_pairs={{0,4},{1,5},{2,3},{3,2},{4,0},{5,1},{6,7},{7,6},{8,12},{9,13},{10,... | collective-permute-start | bytes 24584 | tf_op jit(solution)/shard_map/ppermute | solution.py:470
